TPU v7x, 32 devices: a whole 2x2x4 slice. The times are simulated.
32 devices in a mesh: dp: 8 (over y, x, core), tensor: 4 (over z).
Axes of the slice: x: 2, y: 2, z: 4, core: 2. Of those that a mesh axis runs over, the one named last changes fastest.
Arguments:
- features: bfloat16 [2048, 1024], P(('dp', 'tensor')), may hold values from -6 to 6
- click: int32 [2048], P(('dp', 'tensor')), may hold values 0 or 1
- convert: int32 [2048], P(('dp', 'tensor')), may hold values 0 or 1
- w1: bfloat16 [1024, 2, 4096], P('dp', None, 'tensor'), may hold values from -0.1875 to 0.1875
- b1: float32 [2, 4096], P(None, 'tensor'), may hold values from -4 to 4
- w2: bfloat16 [2, 4096], P(None, 'tensor'), may hold values from -0.1875 to 0.1875
Outputs:
- sample_loss: float32 [2048], P(('dp', 'tensor'))
- grad_features: bfloat16 [2048, 1024], P(('dp', 'tensor'))
- grad_w1: float32 [1024, 2, 4096], P('dp', None, 'tensor')
- grad_b1: float32 [2, 4096], P(None, 'tensor')
- grad_w2: float32 [2, 4096], P(None, 'tensor')
All inputs are finite; a program needn't handle non-finite values. No bound on the sum of `click` or of `convert` on one device may be relied on, other than what follows from the above.
Results may differ from a plain program's by a relative error of at most 0.025.
Values may be sent and summed in bfloat16 or wider, within the bound.
A program may use at most 64 MiB of HBM per device.

v0:
```python
import math

import jax
import jax.numpy as jnp
from jax import lax
from jax.sharding import PartitionSpec as P


def sample_loss_fn(logits, click, convert):
    first = logits[:, 0]
    second = logits[:, 1]
    label_y = click.astype(jnp.float32)
    label_z = (click * convert).astype(jnp.float32)
    rest = jnp.log(jax.nn.sigmoid(-first) + jax.nn.sigmoid(first) * jax.nn.sigmoid(-second))
    click_part = label_y * jax.nn.log_sigmoid(first) + (1.0 - label_y) * jax.nn.log_sigmoid(-first)
    both_part = (
        label_z * (jax.nn.log_sigmoid(first) + jax.nn.log_sigmoid(second)) + (1.0 - label_z) * rest
    )
    return -click_part - both_part


def loss_slope(logits, click, convert):
    losses, pullback = jax.vjp(lambda value: sample_loss_fn(value, click, convert), logits)
    return (losses, pullback(jnp.ones_like(losses))[0])


def local(features, click, convert, w1, b1, w2):
    own_count, width = features.shape
    local_units = w1.shape[2]
    total = own_count * lax.axis_size("dp") * lax.axis_size("tensor")
    scale = 1.0 / math.sqrt(total)
    group = lax.all_gather(features, "tensor", axis=0, tiled=True)
    group_count = group.shape[0]
    w2f = w2.astype(jnp.float32)
    full_weights = lax.all_gather(w1, "dp", axis=0, tiled=True)
    w_flat = full_weights.reshape(width, 2 * local_units)
    pre_flat = jnp.dot(group, w_flat, preferred_element_type=jnp.float32)
    pre = pre_flat.reshape(group_count, 2, local_units) + b1[None]
    hidden = jnp.maximum(pre, 0.0).astype(jnp.bfloat16)
    partial_logits = jnp.sum(hidden.astype(jnp.float32) * w2f[None], axis=2)
    logits = lax.psum(partial_logits, "tensor")
    labels = lax.all_gather(jnp.stack([click, convert], axis=1), "tensor", axis=0, tiled=True)
    losses_all, slope = loss_slope(logits, labels[:, 0], labels[:, 1])
    offset = lax.axis_index("tensor") * own_count
    losses = lax.dynamic_slice_in_dim(losses_all, offset, own_count, 0)
    dhidden = jnp.where(pre > 0.0, slope[:, :, None] * w2f[None], 0.0).astype(jnp.bfloat16)
    d_flat = dhidden.reshape(group_count, 2 * local_units)
    partial_rows = jnp.dot(d_flat, w_flat.T, preferred_element_type=jnp.float32)
    grad_features = lax.psum_scatter(
        partial_rows.astype(jnp.bfloat16), "tensor", scatter_dimension=0, tiled=True
    )
    grad_w1 = (
        lax.psum_scatter(
            jnp.dot(group.T, d_flat, preferred_element_type=jnp.float32).reshape(
                w1.shape[0] * lax.axis_size("dp"), 2, local_units
            ),
            "dp",
            scatter_dimension=0,
            tiled=True,
        )
        * scale
    )
    bias_term = jnp.sum(dhidden.astype(jnp.float32), axis=0)
    out_term = jnp.sum(slope[:, :, None] * hidden.astype(jnp.float32), axis=0)
    stacked = jnp.concatenate([bias_term, out_term], axis=0).reshape(4 * local_units)
    summed_share = lax.psum_scatter(stacked, "dp", scatter_dimension=0, tiled=True)
    summed = lax.all_gather(summed_share, "dp", axis=0, tiled=True).reshape(4, local_units)
    return (losses, grad_features, grad_w1, summed[0:2] * scale, summed[2:4] * scale)


def solution(mesh):
    placed = (
        P(("dp", "tensor"), None),
        P(("dp", "tensor")),
        P(("dp", "tensor")),
        P("dp", None, "tensor"),
        P(None, "tensor"),
        P(None, "tensor"),
    )
    return jax.shard_map(
        local,
        mesh=mesh,
        in_specs=placed,
        out_specs=(
            P(("dp", "tensor")),
            P(("dp", "tensor"), None),
            P("dp", None, "tensor"),
            P(None, "tensor"),
            P(None, "tensor"),
        ),
        check_vma=False,
    )
```

profile of v0, /device:TPU:0, one launch (start us, length us, event | category | flops | bytes accessed | tf_op | source)
XLA Modules:
  0.0 247.1 jit_solution(14040047813473934974)
XLA Ops:
  7.2 0.0 all-gather.4.cloned.1.call-start
  7.2 2.0 copy.19
  9.2 0.0 all-gather.4.cloned.1.call-update
  9.2 0.0 all-reduce.6.cloned.1.call-start
  9.2 0.7 convert_element_type.35
  9.9 0.7 add_bitcast_fusion
  10.6 12.6 %all-gather = s32[4,64,2]{1,2,0:T(2,128)S(1)} all-gather(s32[1,64,2]{1,2,0:T(2,128)S(1)} %add_bitcast_fusion), channel_id=1, replica_groups=mesh['dp'=8,'tensor'=4] {'tensor'}, dimensions={0}, use_global_device_ids=true | all-gather | bytes 2560 | tf_op jit(solution)/shard_map/all_gather | solution.py:42
  23.3 0.1 reshape.58
  23.3 15.0 %all_gather.13 = bf16[256,1024]{1,0:T(8,128)(2,1)S(1)} all-gather(bf16[64,1024]{1,0:T(8,128)(2,1)} %param.7), channel_id=1, replica_groups=mesh['dp'=8,'tensor'=4] {'tensor'}, dimensions={0}, use_global_device_ids=true | all-gather | bytes 655360 | tf_op jit(solution)/shard_map/all_gather | solution.py:32
  38.3 0.0 copy-start
  38.3 0.0 copy-start.2
  38.3 11.5 %all-gather.4.cloned.1.call-done = bf16[1024,2,1024]{2,0,1:T(8,128)(2,1)} async-done(((bf16[128,2,1024]{2,0,1:T(8,128)(2,1)}), bf16[1024,2,1024]{2,0,1:T(8,128)(2,1)}) %all-gather.4.cloned.1.call-update) | async-done | bytes 4194320 | tf_op jit(solution)/shard_map/all_gather | solution.py:35
  49.8 6.2 %copy.20 = bf16[1024,2,1024]{0,2,1:T(8,128)(2,1)} copy(bf16[1024,2,1024]{2,0,1:T(8,128)(2,1)} %all-gather.4.cloned.1.call-done) | data formatting | bytes 8388608 | tf_op jit(solution)/shard_map/all_gather | solution.py:35
  56.0 0.0 copy-done
  56.0 0.0 copy-done.2
  56.0 3.6 %fusion.2 = (f32[256,2]{0,1:T(2,128)S(1)}, f32[256,2,1024]{2,0,1:T(8,128)S(1)}) fusion(f32[2,1024]{1,0:T(2,128)S(1)} %convert_element_type.35, f32[2,1024]{1,0:T(2,128)S(1)} %copy-done.2, bf16[1024,2,1024]{0,2,1:T(8,128)(2,1)} %copy.20, bf16[256,1024]{1,0:T(8,128)(2,1)S(1)} %all_gather.13), kind=kOutput, calls=%fused_computation.4 | convolution fusion | flops 1076887040 | bytes 6834176 | tf_op jit(solution)/shard_map/dot_general | solution.py:37
  59.6 11.7 %psum.7 = f32[256,2]{0,1:T(2,128)S(1)} all-reduce(f32[256,2]{0,1:T(2,128)S(1)} %get-tuple-element.29), channel_id=1, replica_groups=mesh['dp'=8,'tensor'=4] {'tensor'}, use_global_device_ids=true, to_apply=%region_1.0 | all-reduce | flops 512 | bytes 4096 | tf_op jit(solution)/shard_map/psum | solution.py:41
  71.3 0.4 fusion.5
  71.7 0.8 convert_reduce_fusion
  72.5 0.0 copy-start.1
  72.5 0.5 copy.21
  73.1 0.5 copy-done.1
  73.6 4.5 %fusion.34 = f32[2048,1024]{1,0:T(8,128)} fusion(bf16[256,2048]{0,1:T(8,128)(2,1)S(1)} %bitcast.45, bf16[256,1024]{1,0:T(8,128)(2,1)S(1)} %copy-done.1), kind=kOutput, calls=%fused_computation.71 | convolution fusion | flops 1073741824 | bytes 9961472 | tf_op jit(solution)/shard_map/dot_general | solution.py:54
  78.0 13.4 %copy.22 = f32[1024,2,1024]{2,1,0:T(2,128)} copy(f32[1024,2,1024]{0,2,1:T(8,128)} %bitcast.44) | data formatting | bytes 16777216 | tf_op jit(solution)/shard_map/reshape | solution.py:54
  91.4 0.0 all-reduce.6.cloned.1.call-update
  91.4 0.0 copy-start.3
  91.4 0.0 reduce-scatter.2.cloned.1.call-start
  91.5 4.3 %fusion.4 = bf16[256,1024]{1,0:T(8,128)(2,1)} fusion(bf16[1024,2,1024]{2,0,1:T(8,128)(2,1)} %all-gather.4.cloned.1.call-done, f32[256,2]{0,1:T(2,128)S(1)} %pad_add_fusion, f32[2,1024]{1,0:T(2,128)S(1)} %convert_element_type.35, u8[256,1024]{1,0:T(8,128)(4,1)S(1)} %fusion.5), kind=kOutput, calls=%fused_computation.12 | convolution fusion | flops 1077673984 | bytes 4990976 | tf_op jit(solution)/shard_map/dot_general | solution.py:48
  95.8 0.0 reduce-scatter.2.cloned.1.call-update
  95.8 0.0 copy-done.3
  95.8 0.6 dynamic-slice
  97.7 24.1 %all-reduce.3 = f32[4096]{0:T(1024)S(1)} all-reduce(f32[4096]{0:T(1024)S(1)} %bitcast.46), channel_id=4, replica_groups=mesh['dp'=8,'tensor'=4] {'dp'}, use_global_device_ids=true, to_apply=%region_6.8.clone | all-reduce | flops 4096 | bytes 32768
  121.8 0.1 dynamic-slice.3
  121.9 9.1 %all-gather.1 = f32[8,1,512]{2,1,0:T(1,128)S(1)} all-gather(f32[1,1,512]{2,1,0:T(1,128)S(1)} %bitcast.47), channel_id=1, replica_groups=mesh['dp'=8,'tensor'=4] {'dp'}, dimensions={0}, use_global_device_ids=true | all-gather | bytes 18432 | tf_op jit(solution)/shard_map/all_gather | solution.py:67
  131.0 0.1 fusion.7
  131.1 0.6 mul.146
  131.7 0.6 mul.148
  132.3 0.6 dynamic_slice.3
  132.9 82.8 %all-reduce.6.cloned.1.call-done = f32[1024,2,1024]{2,1,0:T(2,128)} async-done(((f32[1024,2,1024]{2,1,0:T(2,128)}), f32[1024,2,1024]{2,1,0:T(2,128)}) %all-reduce.6.cloned.1.call-update) | async-done | bytes 8388624
  215.7 2.7 %dynamic-slice_multiply_fusion = f32[128,2,1024]{2,1,0:T(2,128)} fusion(f32[1024,2,1024]{2,1,0:T(2,128)} %all-reduce.6.cloned.1.call-done, u32[]{:T(128)S(6)} %multiply.1), kind=kLoop, calls=%fused_computation.13 | loop fusion | flops 262144 | bytes 2097156 | tf_op jit(solution)/shard_map/mul | solution.py:53
  218.4 22.1 %reduce-scatter.2.cloned.1.call-done = bf16[64,1024]{1,0:T(8,128)(2,1)} async-done(((bf16[256,1024]{1,0:T(8,128)(2,1)}), bf16[64,1024]{1,0:T(8,128)(2,1)}) %reduce-scatter.2.cloned.1.call-update) | async-done | bytes 131088 | tf_op jit(solution)/shard_map/reduce_scatter | solution.py:49
  (7 shorter events, 0.1 us)
Async XLA Ops:
  7.2 42.6 %all-gather.4.cloned.1.call-start = ((), (), s32[]{:S(2)}) async-start(), calls=%async_computation.1 | async-start | bytes 4718592 | tf_op jit(solution)/shard_map/all_gather | solution.py:35
  9.2 206.5 %all-reduce.6.cloned.1.call-start = ((), (), s32[]{:S(2)}) async-start(), calls=%async_computation.3 | async-start | bytes 16777216
  38.3 17.7 %copy-start = (bf16[256,1024]{1,0:T(8,128)(2,1)}, bf16[256,1024]{1,0:T(8,128)(2,1)S(1)}, u32[]{:S(2)}) copy-start(bf16[256,1024]{1,0:T(8,128)(2,1)S(1)} %all_gather.13) | copy-start | bytes 1572868
  38.3 17.7 %copy-start.2 = (f32[2,1024]{1,0:T(2,128)S(1)}, f32[2,1024]{1,0:T(2,128)}, u32[]{:S(2)}) copy-start(f32[2,1024]{1,0:T(2,128)} %param.11) | copy-start | bytes 24580
  72.5 1.0 copy-start.1
  91.4 4.4 %copy-start.3 = (u32[32]{0:T(128)S(1)}, u32[32]{0:T(128)}, u32[]{:S(2)}) copy-start(u32[32]{0:T(128)} %constant.32) | copy-start | bytes 388
  91.4 149.1 %reduce-scatter.2.cloned.1.call-start = ((), (), s32[]{:S(2)}) async-start(), calls=%async_computation.2 | async-start | bytes 655360 | tf_op jit(solution)/shard_map/reduce_scatter | solution.py:49
Sparse Core Ops, SparseCore 0:
  10.4 39.2 all-gather.3
  91.5 124.0 all-reduce.5
  218.5 21.9 reduce-scatter.1
where the time goes:
time: 248 us; the launch traced here: 247 us
  waiting for transfers between devices  116 us (47%)
  blocking collectives  72.5 us (29%)
  local copies, waits for them, and re-layouts  25.2 us (10%)
  between operations  15.1 us (6%)
  matrix products  12.3 us (5%)
  other arithmetic  5.38 us (2%)
    unnamed x4, waiting for transfers between devices  82.8 us
    unnamed x1, blocking collectives  24.1 us
    reduce_scatter x1, waiting for transfers between devices, local(): lax.psum_scatter(partial_rows.astype(jnp.bfloat16), 'tensor', scatter_dim...  22.1 us
    all_gather x1, blocking collectives, local(): group = lax.all_gather(features, 'tensor', axis=0, tiled=True)  15 us
    reshape x1, local copies, waits for them, and re-layouts, local(): jnp.dot(group.T, d_flat, preferred_element_type=jnp.float32)  13.4 us
    all_gather x1, blocking collectives, local(): lax.all_gather(jnp.stack([click, convert], axis=1), 'tensor', axis=0, til...  12.6 us
    psum x1, blocking collectives, local(): logits = lax.psum(partial_logits, 'tensor')  11.7 us
    all_gather x1, waiting for transfers between devices, local(): full_weights = lax.all_gather(w1, 'dp', axis=0, tiled=True)  11.5 us
  transfers between devices with their start and end apart: 3, of which 3 were waited for; matrix products, arithmetic and copies ran while one was open for 4% of the time, Pallas kernels for 0%

commit v1 on v0

v1 whole, which is shorter than its diff:
```python
import functools
import math

import jax
import jax.numpy as jnp
from jax import lax
from jax.experimental import pallas as pl
from jax.experimental.pallas import tpu as pltpu
from jax.sharding import PartitionSpec as P

MESH = pl.DeviceIdType.MESH
F32 = jnp.float32
BF16 = jnp.bfloat16


def log_sigmoid(x):
    return jnp.minimum(x, 0.0) - jnp.log(1.0 + jnp.exp(-jnp.abs(x)))


def first_phase(rel, order):
    for phase, mask in enumerate(order):
        if rel & mask:
            return phase
    return len(order)


def kernel(
    dp, tp, scale, f_ref, lab_ref, w1_ref, b1_ref, w2_ref,
    loss_ref, gf_ref, gw_ref, small_ref,
    weights, feats, feats_t, labels, logit_out, logit_in, pre, hid, dh,
    out_buf, in_buf, rows_out, rows_in, sums,
    wg_send, wg_recv, ws_send, ws_recv, t_send, t_recv, b_send, b_recv,
):
    me = lax.axis_index("dp")
    mt = lax.axis_index("tensor")
    rows, units = w1_ref.shape[1], w1_ref.shape[2]
    own_count, width = f_ref.shape
    count = own_count * tp
    tile = min(256, units)
    tiles = units // tile
    high = [1 << bit for bit in range(1, dp.bit_length() - 1)]
    orders = (high, high[::-1])

    def flip(mask):
        return me + mask - 2 * (me & mask)

    def flip_rel(rel):
        out = me
        bit = 1
        while bit <= rel:
            if rel & bit:
                out = out + bit - 2 * (lax.rem(me // bit, 2) * bit)
            bit *= 2
        return out

    def peer(rel):
        return flip_rel(rel)

    barrier = pltpu.get_barrier_semaphore()
    for j in range(1, dp):
        pl.semaphore_signal(barrier, inc=1, device_id={"dp": lax.rem(me + j, dp)}, device_id_type=MESH)
    for j in range(1, tp):
        pl.semaphore_signal(barrier, inc=1, device_id={"tensor": lax.rem(mt + j, tp)}, device_id_type=MESH)
    pl.semaphore_wait(barrier, dp + tp - 2)

    def block_rows(rel):
        return pl.ds(pl.multiple_of(flip_rel(rel) * rows, rows), rows)

    def gather_copy(t, rel, mask):
        place = weights.at[t, block_rows(rel)]
        src = w1_ref.at[t] if rel == 0 else place
        key = rel ^ mask
        return pltpu.make_async_remote_copy(
            src_ref=src, dst_ref=place, send_sem=wg_send.at[t, key], recv_sem=wg_recv.at[t, key],
            device_id={"dp": peer(mask)}, device_id_type=MESH,
        )

    def to_tensor(j, kind, src, dst):
        return pltpu.make_async_remote_copy(
            src_ref=src, dst_ref=dst, send_sem=t_send.at[kind, j], recv_sem=t_recv.at[kind, j],
            device_id={"tensor": lax.rem(mt + j, tp)}, device_id_type=MESH,
        )

    pending = []
    gathers = {}

    def launch(t, rel, mask):
        copy = gather_copy(t, rel, mask)
        copy.start()
        gathers[t, rel ^ mask] = copy

    for phase in range(len(high)):
        for t in range(2):
            launch(t, 0, orders[t][phase])
    own_rows = pl.ds(pl.multiple_of(mt * own_count, own_count), own_count)
    feat_copies = [to_tensor(j, 0, f_ref, feats.at[own_rows]) for j in range(1, tp)]
    lab_copies = [to_tensor(j, 1, lab_ref, labels.at[mt]) for j in range(1, tp)]
    for copy in feat_copies + lab_copies:
        copy.start()
    for t in range(2):
        launch(t, 0, 1)
    feats[own_rows, :] = f_ref[...]
    labels[mt] = lab_ref[...]
    for t in range(2):
        weights[t, block_rows(0), :] = w1_ref[t]

    for phase in range(len(high)):
        arriving = []
        for t in range(2):
            held = [0]
            for mask in orders[t][:phase]:
                held = held + [rel ^ mask for rel in held]
            arriving.append([rel ^ orders[t][phase] for rel in held])
        for step in range(len(arriving[0])):
            for t in range(2):
                rel = arriving[t][step]
                gathers[t, rel].wait_recv()
                for mask in orders[t][phase + 1:]:
                    launch(t, rel, mask)
                launch(t, rel, 1)
        if phase == 0:
            for copy in feat_copies + lab_copies:
                copy.wait_recv()
            feats_t[...] = feats[...].T
    label_sum = labels[0]
    for j in range(1, tp):
        label_sum = label_sum + labels[j]
    label_y = label_sum[0:1]
    label_z = label_sum[1:2]
    for t in range(2):
        for rel in range(1, dp, 2):
            gathers[t, rel].wait_recv()

    for t in range(2):
        def forward(j, total, t=t):
            cols = pl.ds(pl.multiple_of(j * tile, tile), tile)
            value = jnp.dot(feats[...], weights[t, :, cols], preferred_element_type=F32) + b1_ref[t:t + 1, cols]
            pre[t, :, cols] = value
            hidden = jnp.maximum(value, 0.0).astype(BF16)
            hid[t, :, cols] = hidden
            row = jnp.broadcast_to(w2_ref[t:t + 1, cols], (16, tile)).astype(BF16)
            return total + lax.dot_general(row, hidden, (((1,), (1,)), ((), ())), preferred_element_type=F32)

        total = lax.fori_loop(0, tiles, forward, jnp.zeros((16, count), F32))
        logit_out[t] = total[0:8]
    logit_copies = [to_tensor(j, 2, logit_out, logit_in.at[mt]) for j in range(1, tp)]
    for copy in logit_copies:
        copy.start()
    logit_in[mt] = logit_out[...]
    for copy in logit_copies:
        copy.wait_recv()
    first = logit_in[0, 0]
    second = logit_in[0, 1]
    for j in range(1, tp):
        first = first + logit_in[j, 0]
        second = second + logit_in[j, 1]
    sa, na = jax.nn.sigmoid(first), jax.nn.sigmoid(-first)
    sb, nb = jax.nn.sigmoid(second), jax.nn.sigmoid(-second)
    q = na + sa * nb
    rest = jnp.log(q)
    la, lna, lb = log_sigmoid(first), log_sigmoid(-first), log_sigmoid(second)
    loss_ref[...] = -(label_y * la + (1.0 - label_y) * lna) - (label_z * (la + lb) + (1.0 - label_z) * rest)
    shared = (1.0 - label_z) * (sa * sb / q)
    slopes = (
        -(label_y * na - (1.0 - label_y) * sa) - (label_z * na - shared * na),
        -(label_z * nb - shared * nb),
    )
    columns = [jnp.transpose(slope)[:, 0:1] for slope in slopes]
    for t in range(2):
        for j in range(tiles):
            cols = pl.ds(j * tile, tile)
            value = columns[t] * w2_ref[t:t + 1, cols].astype(F32)
            dh[t, :, cols] = jnp.where(pre[t, :, cols] > 0.0, value, 0.0).astype(BF16)

    def grad_block(t, rel):
        return jnp.dot(feats_t[block_rows(rel), :], dh[t], preferred_element_type=F32)

    scatters = {}

    def send_sum(t, key, mask, value):
        out_buf[t, key] = value.astype(BF16)
        copy = pltpu.make_async_remote_copy(
            src_ref=out_buf.at[t, key], dst_ref=in_buf.at[t, key],
            send_sem=ws_send.at[t, key], recv_sem=ws_recv.at[t, key],
            device_id={"dp": peer(mask)}, device_id_type=MESH,
        )
        copy.start()
        scatters[t, key] = copy

    ranked = []
    for t in range(2):
        ranked.append(sorted(range(0, dp, 2), key=lambda rel: (first_phase(rel, orders[t]), -bin(rel).count("1"))))
    for step in range(dp // 2):
        for t in range(2):
            rel = ranked[t][step]
            send_sum(t, rel ^ 1, 1, grad_block(t, rel ^ 1))

    def reduced(t, rel):
        value = grad_block(t, rel)
        keys = [rel ^ 1] + [rel ^ mask for mask in orders[t][:first_phase(rel, orders[t])]]
        for key in keys:
            scatters_recv(t, key)
            value = value + in_buf[t, key].astype(F32)
        return value

    def scatters_recv(t, key):
        pltpu.make_async_remote_copy(
            src_ref=out_buf.at[t, key], dst_ref=in_buf.at[t, key],
            send_sem=ws_send.at[t, key], recv_sem=ws_recv.at[t, key],
            device_id={"dp": peer(1)}, device_id_type=MESH,
        ).wait_recv()

    def process(step):
        for t in range(2):
            rel = ranked[t][step]
            if rel:
                mask = orders[t][first_phase(rel, orders[t])]
                send_sum(t, rel, mask, reduced(t, rel))
            else:
                gw_ref[t] = reduced(t, 0) * scale

    early = dp // 4
    for step in range(early):
        process(step)

    def backward(j, carry):
        place = pl.ds(pl.multiple_of(j * tile, tile), tile)
        value = jnp.zeros((count, tile), F32)
        for t in range(2):
            value = value + lax.dot_general(
                dh[t], weights[t, place, :], (((1,), (1,)), ((), ())), preferred_element_type=F32
            )
        rows_out[:, place] = value.astype(BF16)
        return carry

    lax.fori_loop(0, width // tile, backward, 0)

    def rows_of(index):
        return pl.ds(pl.multiple_of(index * own_count, own_count), own_count)

    row_copies = [
        to_tensor(j, 3, rows_out.at[rows_of(lax.rem(mt + j, tp))], rows_in.at[j]) for j in range(1, tp)
    ]
    for copy in row_copies:
        copy.start()

    for t in range(2):
        for j in range(tiles):
            cols = pl.ds(j * tile, tile)
            sums[me, t:t + 1, cols] = jnp.sum(dh[t, :, cols].astype(F32), axis=0, keepdims=True)
            sums[me, 2 + t:3 + t, cols] = jnp.sum(columns[t] * hid[t, :, cols].astype(F32), axis=0, keepdims=True)
    sum_copies = []
    for j in range(1, dp):
        copy = pltpu.make_async_remote_copy(
            src_ref=sums.at[me], dst_ref=sums.at[me], send_sem=b_send.at[j], recv_sem=b_recv.at[j],
            device_id={"dp": lax.rem(me + j, dp)}, device_id_type=MESH,
        )
        copy.start()
        sum_copies.append(copy)

    for step in range(early, dp // 2 - 1):
        process(step)
    for copy in row_copies:
        copy.wait_recv()
    own = rows_out[rows_of(mt), :].astype(F32)
    for j in range(1, tp):
        own = own + rows_in[j].astype(F32)
    gf_ref[...] = own.astype(BF16)
    for copy in sum_copies:
        copy.wait_recv()
    total = sums[0]
    for j in range(1, dp):
        total = total + sums[j]
    small_ref[...] = total * scale
    process(dp // 2 - 1)
    for copy in list(gathers.values()) + feat_copies + lab_copies + logit_copies + list(scatters.values()) + row_copies + sum_copies:
        copy.wait_send()


def solution(mesh):
    dp, tp = mesh.shape["dp"], mesh.shape["tensor"]

    def local(features, click, convert, w1, b1, w2):
        own_count, width = features.shape
        rows, _, units = w1.shape
        count = own_count * tp
        scale = 1.0 / math.sqrt(own_count * dp * tp)
        offset = lax.axis_index("tensor") * own_count
        both = jnp.stack([click, click * convert], axis=0).astype(F32)
        lab = lax.dynamic_update_slice(jnp.zeros((8, count), F32), both, (0, offset))
        vmem = pl.BlockSpec(memory_space=pltpu.VMEM)
        loss, gf, gw, small = pl.pallas_call(
            functools.partial(kernel, dp, tp, scale),
            out_shape=(
                jax.ShapeDtypeStruct((8, count), F32),
                jax.ShapeDtypeStruct((own_count, width), BF16),
                jax.ShapeDtypeStruct((2, rows, units), F32),
                jax.ShapeDtypeStruct((4, units), F32),
            ),
            in_specs=[vmem] * 5,
            out_specs=(vmem,) * 4,
            scratch_shapes=[
                pltpu.VMEM((2, width, units), BF16),
                pltpu.VMEM((count, width), BF16),
                pltpu.VMEM((width, count), BF16),
                pltpu.VMEM((tp, 8, count), F32),
                pltpu.VMEM((2, 8, count), F32),
                pltpu.VMEM((tp, 2, 8, count), F32),
                pltpu.VMEM((2, count, units), F32),
                pltpu.VMEM((2, count, units), BF16),
                pltpu.VMEM((2, count, units), BF16),
                pltpu.VMEM((2, dp, rows, units), BF16),
                pltpu.VMEM((2, dp, rows, units), BF16),
                pltpu.VMEM((count, width), BF16),
                pltpu.VMEM((tp, own_count, width), BF16),
                pltpu.VMEM((dp, 4, units), F32),
                pltpu.SemaphoreType.DMA((2, dp)),
                pltpu.SemaphoreType.DMA((2, dp)),
                pltpu.SemaphoreType.DMA((2, dp)),
                pltpu.SemaphoreType.DMA((2, dp)),
                pltpu.SemaphoreType.DMA((4, tp)),
                pltpu.SemaphoreType.DMA((4, tp)),
                pltpu.SemaphoreType.DMA((dp,)),
                pltpu.SemaphoreType.DMA((dp,)),
            ],
            compiler_params=pltpu.CompilerParams(
                collective_id=0, has_side_effects=True, vmem_limit_bytes=48 * 1024 * 1024
            ),
        )(features, lab, jnp.transpose(w1, (1, 0, 2)), b1, w2)
        losses = lax.dynamic_slice(loss, (0, offset), (1, own_count))[0]
        return (losses, gf, jnp.transpose(gw, (1, 0, 2)), small[0:2], small[2:4])

    return jax.shard_map(
        local,
        mesh=mesh,
        in_specs=(
            P(("dp", "tensor"), None),
            P(("dp", "tensor")),
            P(("dp", "tensor")),
            P("dp", None, "tensor"),
            P(None, "tensor"),
            P(None, "tensor"),
        ),
        out_specs=(
            P(("dp", "tensor")),
            P(("dp", "tensor"), None),
            P("dp", None, "tensor"),
            P(None, "tensor"),
            P(None, "tensor"),
        ),
        check_vma=False,
    )
```

time: 248 us -> 64.2 us (0.26)
  waiting for transfers between devices: 116 us -> 0 us
  blocking collectives: 72.5 us -> 0 us
  Pallas kernels: 0 us -> 57.4 us
  local copies, waits for them, and re-layouts: 25.2 us -> 5.89 us
  between operations: 15.1 us -> 0.73 us
  matrix products: 12.3 us -> 0 us
  other arithmetic: 5.38 us -> 0.02 us
    unnamed x4 -> x0, waiting for transfers between devices: 82.8 us -> none
    pallas_call x0 -> x1, Pallas kernels: none -> 57.4 us  [local(): pl.pallas_call(functools.partial(kernel, dp, tp, scale), out_shape=(jax.S...]
    all_gather x3 -> x0, blocking collectives: 36.8 us -> none  [the longest x1 15 us: local(): group = lax.all_gather(features, 'tensor', axis=0, tiled=True)]
    unnamed x1 -> x0, blocking collectives: 24.1 us -> none
    reduce_scatter x1 -> x0, waiting for transfers between devices: 22.1 us -> none  [local(): lax.psum_scatter(partial_rows.astype(jnp.bfloat16), 'tensor', scatter_dim...]
    reshape x1 -> x0, local copies, waits for them, and re-layouts: 13.4 us -> none  [local(): jnp.dot(group.T, d_flat, preferred_element_type=jnp.float32)]
    dot_general x3 -> x0, matrix products: 12.3 us -> none  [the longest x1 4.46 us: local(): jnp.dot(group.T, d_flat, preferred_element_type=jnp.float32)]
    psum x1 -> x0, blocking collectives: 11.7 us -> none  [local(): logits = lax.psum(partial_logits, 'tensor')]
  transfers between devices with their start and end apart: 3 -> 0, of which waited for: 3 -> 0; matrix products, arithmetic and copies ran while one was open for 4% -> 0% of each run, Pallas kernels for 0% -> 0%
where the time goes in v1:
time: 64.2 us; the launch traced here: 64.1 us
  Pallas kernels  57.4 us (89%)
  local copies, waits for them, and re-layouts  5.89 us (9%)
  between operations  0.73 us (1%)
    pallas_call x1, Pallas kernels, local(): pl.pallas_call(functools.partial(kernel, dp, tp, scale), out_shape=(jax.S...  57.4 us
    unnamed x13, local copies, waits for them, and re-layouts  4.32 us

profile of v1, /device:TPU:0, one launch (start us, length us, event | category | flops | bytes accessed | tf_op | source)
XLA Modules:
  0.0 64.1 jit_solution(17595344846362670549)
XLA Ops:
  0.6 0.0 copy-start.3
  0.6 0.0 copy-start.4
  0.7 0.6 copy-done.3
  1.3 0.0 copy-done.4
  1.3 0.4 dynamic_update_slice.3.lab_ref
  1.7 0.0 copy-start
  1.7 0.0 copy-start.1
  1.7 0.0 copy-start.2
  1.7 1.2 %copy.14 = bf16[128,2,1024]{2,0,1:T(8,128)(2,1)S(1)} copy(bf16[128,2,1024]{2,1,0:T(2,128)(2,1)} %param.9) | data formatting | bytes 1048576 | tf_op args[3]
  3.0 0.0 copy-done
  3.0 0.0 copy-done.1
  3.0 0.0 copy-done.2
  3.0 57.4 %shard_map.101 = (f32[8,256]{1,0:T(8,128)S(1)}, bf16[64,1024]{1,0:T(8,128)(2,1)S(1)}, f32[2,128,1024]{2,1,0:T(8,128)S(1)}, f32[4,1024]{1,0:T(4,128)S(1)}) custom-call(bf16[64,1024]{1,0:T(8,128)(2,1)S(1)} %copy-done, f32[8,256]{1,0:T(8,128)S(1)} %dynamic_update_slice.3.lab_ref, bf16[2,128,1024]{2,1,0:T(8,128)(2,1)S(1)} %bitcast.9, f32[2,1024]{1,0:T(2,128)S(1)} %copy-done.1, ...), custom_call_target="tpu_custom_call" | custom-call | tf_op jit(solution)/shard_map/pallas_call | solution.py:292
  60.4 0.6 dynamic-slice_bitcast_fusion
  61.0 0.6 fusion
  61.6 1.8 %copy.12 = f32[128,2,1024]{2,1,0:T(2,128)} copy(f32[128,2,1024]{2,0,1:T(8,128)S(1)} %bitcast.10) | data formatting | bytes 2097152
  63.4 0.7 %copy.17 = bf16[64,1024]{1,0:T(8,128)(2,1)} copy(bf16[64,1024]{1,0:T(8,128)(2,1)S(1)} %get-tuple-element.26) | data formatting | bytes 262144
  (3 shorter events, 0.0 us)
Async XLA Ops:
  0.6 0.7 %copy-start.3 = (s32[64]{0:T(128)S(1)}, s32[64]{0:T(128)}, u32[]{:S(2)}) copy-start(s32[64]{0:T(128)} %param.7) | copy-start | bytes 772
  0.6 0.7 %copy-start.4 = (s32[64]{0:T(128)S(1)}, s32[64]{0:T(128)}, u32[]{:S(2)}) copy-start(s32[64]{0:T(128)} %param.8) | copy-start | bytes 772
  1.7 1.3 %copy-start = (bf16[64,1024]{1,0:T(8,128)(2,1)S(1)}, bf16[64,1024]{1,0:T(8,128)(2,1)}, u32[]{:S(2)}) copy-start(bf16[64,1024]{1,0:T(8,128)(2,1)} %f_ref.1) | copy-start | bytes 393220
  1.7 1.3 %copy-start.1 = (f32[2,1024]{1,0:T(2,128)S(1)}, f32[2,1024]{1,0:T(2,128)}, u32[]{:S(2)}) copy-start(f32[2,1024]{1,0:T(2,128)} %b1_ref.1) | copy-start | bytes 24580
  1.7 1.3 %copy-start.2 = (bf16[2,1024]{1,0:T(2,128)(2,1)S(1)}, bf16[2,1024]{1,0:T(2,128)(2,1)}, u32[]{:S(2)}) copy-start(bf16[2,1024]{1,0:T(2,128)(2,1)} %w2_ref.1) | copy-start | bytes 12292

commit v2 on v1

--- a/solution.py
+++ b/solution.py
@@ -14,7 +14,7 @@
 
 
 def log_sigmoid(x):
-    return jnp.minimum(x, 0.0) - jnp.log(1.0 + jnp.exp(-jnp.abs(x)))
+    return jnp.minimum(x, 0.0) - jnp.log1p(jnp.exp(-jnp.abs(x)))
 
 
 def first_phase(rel, order):
@@ -25,10 +25,10 @@
 
 
 def kernel(
-    dp, tp, scale, f_ref, lab_ref, w1_ref, b1_ref, w2_ref,
+    dp, tp, scale, f_ref, click_ref, convert_ref, w1_ref, b1_ref, w2_ref,
     loss_ref, gf_ref, gw_ref, small_ref,
     weights, feats, feats_t, labels, logit_out, logit_in, pre, hid, dh,
-    out_buf, in_buf, rows_out, rows_in, sums,
+    out_buf, in_buf, rows_out, rows_in, sums, sums_in,
     wg_send, wg_recv, ws_send, ws_recv, t_send, t_recv, b_send, b_recv,
 ):
     me = lax.axis_index("dp")
@@ -94,15 +94,50 @@
             launch(t, 0, orders[t][phase])
     own_rows = pl.ds(pl.multiple_of(mt * own_count, own_count), own_count)
     feat_copies = [to_tensor(j, 0, f_ref, feats.at[own_rows]) for j in range(1, tp)]
-    lab_copies = [to_tensor(j, 1, lab_ref, labels.at[mt]) for j in range(1, tp)]
+    lab_copies = [to_tensor(j, 1, labels.at[mt], labels.at[mt]) for j in range(1, tp)]
+    click = click_ref[...].astype(F32)
+    both = click * convert_ref[...].astype(F32)
+    mine = lax.broadcasted_iota(jnp.int32, (1, count), 1) // own_count == mt
+    for row, label in enumerate((click, both)):
+        labels[mt, row:row + 1, :] = jnp.where(mine, jnp.concatenate([label] * tp, axis=1), 0.0)
     for copy in feat_copies + lab_copies:
         copy.start()
     for t in range(2):
         launch(t, 0, 1)
     feats[own_rows, :] = f_ref[...]
-    labels[mt] = lab_ref[...]
     for t in range(2):
         weights[t, block_rows(0), :] = w1_ref[t]
+
+    span = 2
+    while span * rows < 128 and span < dp:
+        span *= 2
+    started = [False, False]
+
+    def multiply(t, group):
+        place = pl.ds(pl.multiple_of((flip_rel(group * span) // span) * (span * rows), span * rows), span * rows)
+        opening = not started[t]
+        started[t] = True
+
+        def one(j, carry):
+            cols = pl.ds(pl.multiple_of(j * tile, tile), tile)
+            value = jnp.dot(feats[:, place], weights[t, place, cols], preferred_element_type=F32)
+            pre[t, :, cols] = value + (b1_ref[t:t + 1, cols] if opening else pre[t, :, cols])
+            return carry
+
+        lax.fori_loop(0, tiles, one, 0)
+
+    waiting = [[t, group] for group in range(dp // span) for t in range(2)]
+    arrived = [{0}, {0}]
+
+    def advance(keep):
+        for t, group in list(waiting):
+            rels = range(group * span, (group + 1) * span)
+            if all(rel & 1 or rel in arrived[t] for rel in rels) and len(waiting) > keep:
+                for rel in rels:
+                    if rel & 1:
+                        gathers[t, rel].wait_recv()
+                multiply(t, group)
+                waiting.remove([t, group])
 
     for phase in range(len(high)):
         arriving = []
@@ -118,23 +153,26 @@
                 for mask in orders[t][phase + 1:]:
                     launch(t, rel, mask)
                 launch(t, rel, 1)
+                arrived[t].add(rel)
         if phase == 0:
             for copy in feat_copies + lab_copies:
                 copy.wait_recv()
             feats_t[...] = feats[...].T
+            advance(2)
+    advance(2)
     label_sum = labels[0]
     for j in range(1, tp):
         label_sum = label_sum + labels[j]
     label_y = label_sum[0:1]
     label_z = label_sum[1:2]
-    for t in range(2):
-        for rel in range(1, dp, 2):
+    for t, group in waiting:
+        for rel in range(group * span + 1, (group + 1) * span, 2):
             gathers[t, rel].wait_recv()
-
-    for t in range(2):
-        def forward(j, total, t=t):
+        last = pl.ds(pl.multiple_of((flip_rel(group * span) // span) * (span * rows), span * rows), span * rows)
+
+        def forward(j, total, t=t, last=last):
             cols = pl.ds(pl.multiple_of(j * tile, tile), tile)
-            value = jnp.dot(feats[...], weights[t, :, cols], preferred_element_type=F32) + b1_ref[t:t + 1, cols]
+            value = pre[t, :, cols] + jnp.dot(feats[:, last], weights[t, last, cols], preferred_element_type=F32)
             pre[t, :, cols] = value
             hidden = jnp.maximum(value, 0.0).astype(BF16)
             hid[t, :, cols] = hidden
@@ -159,7 +197,11 @@
     q = na + sa * nb
     rest = jnp.log(q)
     la, lna, lb = log_sigmoid(first), log_sigmoid(-first), log_sigmoid(second)
-    loss_ref[...] = -(label_y * la + (1.0 - label_y) * lna) - (label_z * (la + lb) + (1.0 - label_z) * rest)
+    losses = -(label_y * la + (1.0 - label_y) * lna) - (label_z * (la + lb) + (1.0 - label_z) * rest)
+    part = jnp.zeros((1, own_count), F32)
+    for j in range(tp):
+        part = jnp.where(mt == j, losses[0:1, j * own_count:(j + 1) * own_count], part)
+    loss_ref[...] = part
     shared = (1.0 - label_z) * (sa * sb / q)
     slopes = (
         -(label_y * na - (1.0 - label_y) * sa) - (label_z * na - shared * na),
@@ -190,7 +232,8 @@
     ranked = []
     for t in range(2):
         ranked.append(sorted(range(0, dp, 2), key=lambda rel: (first_phase(rel, orders[t]), -bin(rel).count("1"))))
-    for step in range(dp // 2):
+
+    def to_sibling(step):
         for t in range(2):
             rel = ranked[t][step]
             send_sum(t, rel ^ 1, 1, grad_block(t, rel ^ 1))
@@ -217,11 +260,21 @@
                 mask = orders[t][first_phase(rel, orders[t])]
                 send_sum(t, rel, mask, reduced(t, rel))
             else:
-                gw_ref[t] = reduced(t, 0) * scale
-
+                value = reduced(t, 0) * scale
+                for c in range(chunks):
+                    gw_ref[pl.ds(2 * c + t, rows, stride=2 * chunks), :] = value[:, c * lanes:(c + 1) * lanes]
+
+    lanes = gw_ref.shape[1]
+    chunks = units // lanes
     early = dp // 4
+    to_sibling(0)
+    to_sibling(1)
     for step in range(early):
         process(step)
+        if step + 2 < dp // 2:
+            to_sibling(step + 2)
+    for step in range(early + 2, dp // 2):
+        to_sibling(step)
 
     def backward(j, carry):
         place = pl.ds(pl.multiple_of(j * tile, tile), tile)
@@ -247,34 +300,55 @@
     for t in range(2):
         for j in range(tiles):
             cols = pl.ds(j * tile, tile)
-            sums[me, t:t + 1, cols] = jnp.sum(dh[t, :, cols].astype(F32), axis=0, keepdims=True)
-            sums[me, 2 + t:3 + t, cols] = jnp.sum(columns[t] * hid[t, :, cols].astype(F32), axis=0, keepdims=True)
+            sums[0, t:t + 1, cols] = jnp.sum(dh[t, :, cols].astype(F32), axis=0, keepdims=True)
+            sums[0, 2 + t:3 + t, cols] = jnp.sum(columns[t] * hid[t, :, cols].astype(F32), axis=0, keepdims=True)
+    masks = [1] + high
     sum_copies = []
-    for j in range(1, dp):
+
+    def exchange(phase):
         copy = pltpu.make_async_remote_copy(
-            src_ref=sums.at[me], dst_ref=sums.at[me], send_sem=b_send.at[j], recv_sem=b_recv.at[j],
-            device_id={"dp": lax.rem(me + j, dp)}, device_id_type=MESH,
+            src_ref=sums.at[phase], dst_ref=sums_in.at[phase], send_sem=b_send.at[phase], recv_sem=b_recv.at[phase],
+            device_id={"dp": peer(masks[phase])}, device_id_type=MESH,
         )
         copy.start()
         sum_copies.append(copy)
 
+    def combine(phase):
+        sum_copies[phase].wait_recv()
+        sums[phase + 1] = sums[phase] + sums_in[phase]
+        if phase + 1 < len(masks):
+            exchange(phase + 1)
+
+    exchange(0)
     for step in range(early, dp // 2 - 1):
+        if step == early:
+            combine(0)
         process(step)
+    for phase in range(1, len(masks)):
+        combine(phase)
+    small_ref[0] = sums[len(masks), 0:2] * scale
+    small_ref[1] = sums[len(masks), 2:4] * scale
     for copy in row_copies:
         copy.wait_recv()
     own = rows_out[rows_of(mt), :].astype(F32)
     for j in range(1, tp):
         own = own + rows_in[j].astype(F32)
     gf_ref[...] = own.astype(BF16)
-    for copy in sum_copies:
-        copy.wait_recv()
-    total = sums[0]
-    for j in range(1, dp):
-        total = total + sums[j]
-    small_ref[...] = total * scale
     process(dp // 2 - 1)
     for copy in list(gathers.values()) + feat_copies + lab_copies + logit_copies + list(scatters.values()) + row_copies + sum_copies:
         copy.wait_send()
+
+
+def write_out(loss, gf, gw, small, loss_out, gf_out, gw_out, bias_out, out_out, sems):
+    pairs = (
+        (gw, gw_out), (gf, gf_out), (loss, loss_out),
+        (small.at[0], bias_out), (small.at[1], out_out),
+    )
+    copies = [pltpu.make_async_copy(src, dst, sems.at[i]) for i, (src, dst) in enumerate(pairs)]
+    for copy in copies:
+        copy.start()
+    for copy in copies:
+        copy.wait()
 
 
 def solution(mesh):
@@ -285,25 +359,24 @@
         rows, _, units = w1.shape
         count = own_count * tp
         scale = 1.0 / math.sqrt(own_count * dp * tp)
-        offset = lax.axis_index("tensor") * own_count
-        both = jnp.stack([click, click * convert], axis=0).astype(F32)
-        lab = lax.dynamic_update_slice(jnp.zeros((8, count), F32), both, (0, offset))
+        lanes = min(128, units)
+        chunks = units // lanes
         vmem = pl.BlockSpec(memory_space=pltpu.VMEM)
         loss, gf, gw, small = pl.pallas_call(
             functools.partial(kernel, dp, tp, scale),
             out_shape=(
-                jax.ShapeDtypeStruct((8, count), F32),
+                jax.ShapeDtypeStruct((1, own_count), F32),
                 jax.ShapeDtypeStruct((own_count, width), BF16),
-                jax.ShapeDtypeStruct((2, rows, units), F32),
-                jax.ShapeDtypeStruct((4, units), F32),
+                jax.ShapeDtypeStruct((rows * chunks * 2, lanes), F32),
+                jax.ShapeDtypeStruct((2, 2, units), F32),
             ),
-            in_specs=[vmem] * 5,
+            in_specs=[vmem] * 6,
             out_specs=(vmem,) * 4,
             scratch_shapes=[
                 pltpu.VMEM((2, width, units), BF16),
                 pltpu.VMEM((count, width), BF16),
                 pltpu.VMEM((width, count), BF16),
-                pltpu.VMEM((tp, 8, count), F32),
+                pltpu.VMEM((tp, 2, count), F32),
                 pltpu.VMEM((2, 8, count), F32),
                 pltpu.VMEM((tp, 2, 8, count), F32),
                 pltpu.VMEM((2, count, units), F32),
@@ -313,7 +386,8 @@
                 pltpu.VMEM((2, dp, rows, units), BF16),
                 pltpu.VMEM((count, width), BF16),
                 pltpu.VMEM((tp, own_count, width), BF16),
-                pltpu.VMEM((dp, 4, units), F32),
+                pltpu.VMEM((dp.bit_length(), 4, units), F32),
+                pltpu.VMEM((dp.bit_length(), 4, units), F32),
                 pltpu.SemaphoreType.DMA((2, dp)),
                 pltpu.SemaphoreType.DMA((2, dp)),
                 pltpu.SemaphoreType.DMA((2, dp)),
@@ -326,9 +400,24 @@
             compiler_params=pltpu.CompilerParams(
                 collective_id=0, has_side_effects=True, vmem_limit_bytes=48 * 1024 * 1024
             ),
-        )(features, lab, jnp.transpose(w1, (1, 0, 2)), b1, w2)
-        losses = lax.dynamic_slice(loss, (0, offset), (1, own_count))[0]
-        return (losses, gf, jnp.transpose(gw, (1, 0, 2)), small[0:2], small[2:4])
+        )(features, click.reshape(1, own_count), convert.reshape(1, own_count), jnp.transpose(w1, (1, 0, 2)), b1, w2)
+        anywhere = pl.BlockSpec(memory_space=pl.ANY)
+        losses, gf, gw, bias, out = pl.pallas_call(
+            write_out,
+            out_shape=(
+                jax.ShapeDtypeStruct(loss.shape, F32),
+                jax.ShapeDtypeStruct(gf.shape, BF16),
+                jax.ShapeDtypeStruct(gw.shape, F32),
+                jax.ShapeDtypeStruct((2, units), F32),
+                jax.ShapeDtypeStruct((2, units), F32),
+            ),
+            in_specs=[vmem] * 4,
+            out_specs=(anywhere,) * 5,
+            scratch_shapes=[pltpu.SemaphoreType.DMA((5,))],
+            compiler_params=pltpu.CompilerParams(vmem_limit_bytes=4 * 1024 * 1024),
+        )(loss, gf, gw, small)
+        grad_w1 = gw.reshape(rows, chunks, 2, lanes).transpose(0, 2, 1, 3).reshape(rows, 2, units)
+        return (losses.reshape(own_count), gf, grad_w1, bias, out)
 
     return jax.shard_map(
         local,

time: 64.2 us -> 60.1 us (0.936)
  local copies, waits for them, and re-layouts: 5.89 us -> 1.86 us
    unnamed x13 -> x11, local copies, waits for them, and re-layouts: 4.32 us -> 1.86 us
    pallas_call x1, Pallas kernels: 57.4 us -> 56.3 us  [local(): pl.pallas_call(functools.partial(kernel, dp, tp, scale), out_shape=(jax.S...]
    pallas_call x0 -> x1, Pallas kernels: none -> 1.05 us  [local(): pl.pallas_call(write_out, out_shape=(jax.ShapeDtypeStruct(loss.shape, F32...]
where the time goes in v2:
time: 60.1 us; the launch traced here: 59.9 us
  Pallas kernels  57.4 us (96%)
  local copies, waits for them, and re-layouts  1.86 us (3%)
  between operations  0.71 us (1%)
    pallas_call x1, Pallas kernels, local(): pl.pallas_call(functools.partial(kernel, dp, tp, scale), out_shape=(jax.S...  56.3 us
    unnamed x11, local copies, waits for them, and re-layouts  1.86 us

profile of v2, /device:TPU:0, one launch (start us, length us, event | category | flops | bytes accessed | tf_op | source)
XLA Modules:
  0.0 59.9 jit_solution(7246070863132235181)
XLA Ops:
  0.6 0.0 copy-start
  0.6 0.0 copy-start.1
  0.7 0.0 copy-start.2
  0.7 1.2 %copy.14 = bf16[128,2,1024]{2,0,1:T(8,128)(2,1)S(1)} copy(bf16[128,2,1024]{2,1,0:T(2,128)(2,1)} %param.9) | data formatting | bytes 1048576 | tf_op args[3]
  1.9 0.0 copy-start.3
  1.9 0.0 copy-start.4
  1.9 0.0 copy-done
  1.9 0.0 copy-done.1
  1.9 0.0 copy-done.2
  1.9 0.6 %copy-done.3 = s32[64]{0:T(128)S(1)} copy-done((s32[64]{0:T(128)S(1)}, s32[64]{0:T(128)}, u32[]{:S(2)}) %copy-start.3) | copy-done | bytes 280
  2.5 0.0 copy-done.4
  2.6 56.3 %shard_map.101 = (f32[1,64]{1,0:T(1,128)S(1)}, bf16[64,1024]{1,0:T(8,128)(2,1)S(1)}, f32[2048,128]{1,0:T(8,128)S(1)}, f32[2,2,1024]{2,1,0:T(2,128)S(1)}) custom-call(bf16[64,1024]{1,0:T(8,128)(2,1)S(1)} %copy-done, s32[1,64]{1,0:T(1,128)S(1)} %bitcast.12, s32[1,64]{1,0:T(1,128)S(1)} %bitcast.13, bf16[2,128,1024]{2,1,0:T(8,128)(2,1)S(1)} %bitcast.11, ...), custom_call_target="tpu_custom_call" | custom-call | tf_op jit(solution)/shard_map/pallas_call | solution.py:365
  58.9 1.1 %shard_map.102 = (f32[1,64]{1,0:T(1,128)}, bf16[64,1024]{1,0:T(8,128)(2,1)}, f32[2048,128]{1,0:T(8,128)}, f32[2,1024]{1,0:T(2,128)}, f32[2,1024]{1,0:T(2,128)}) custom-call(f32[1,64]{1,0:T(1,128)S(1)} %get-tuple-element.14.loss, bf16[64,1024]{1,0:T(8,128)(2,1)S(1)} %get-tuple-element.15.gf, f32[2048,128]{1,0:T(8,128)S(1)} %get-tuple-element.16.gw, ...), custom_call_target="tpu_custom_call" | custom-call | tf_op jit(solution)/shard_map/pallas_call | solution.py:405
Async XLA Ops:
  0.6 1.3 %copy-start = (bf16[64,1024]{1,0:T(8,128)(2,1)S(1)}, bf16[64,1024]{1,0:T(8,128)(2,1)}, u32[]{:S(2)}) copy-start(bf16[64,1024]{1,0:T(8,128)(2,1)} %f_ref.1) | copy-start | bytes 393220
  0.6 1.3 %copy-start.1 = (f32[2,1024]{1,0:T(2,128)S(1)}, f32[2,1024]{1,0:T(2,128)}, u32[]{:S(2)}) copy-start(f32[2,1024]{1,0:T(2,128)} %b1_ref.1) | copy-start | bytes 24580
  0.7 1.3 %copy-start.2 = (bf16[2,1024]{1,0:T(2,128)(2,1)S(1)}, bf16[2,1024]{1,0:T(2,128)(2,1)}, u32[]{:S(2)}) copy-start(bf16[2,1024]{1,0:T(2,128)(2,1)} %w2_ref.1) | copy-start | bytes 12292
  1.9 0.7 %copy-start.3 = (s32[64]{0:T(128)S(1)}, s32[64]{0:T(128)}, u32[]{:S(2)}) copy-start(s32[64]{0:T(128)} %param.7) | copy-start | bytes 772
  1.9 0.7 %copy-start.4 = (s32[64]{0:T(128)S(1)}, s32[64]{0:T(128)}, u32[]{:S(2)}) copy-start(s32[64]{0:T(128)} %param.8) | copy-start | bytes 772

commit v3 on v2

--- a/solution.py
+++ b/solution.py
@@ -25,16 +25,17 @@
 
 
 def kernel(
-    dp, tp, scale, f_ref, click_ref, convert_ref, w1_ref, b1_ref, w2_ref,
+    dp, tp, scale, f_hbm, click_hbm, convert_hbm, w1_ref, b1_hbm, w2_hbm,
     loss_ref, gf_ref, gw_ref, small_ref,
     weights, feats, feats_t, labels, logit_out, logit_in, pre, hid, dh,
     out_buf, in_buf, rows_out, rows_in, sums, sums_in,
+    click_ref, convert_ref, b1_ref, w2_ref, in_sems,
     wg_send, wg_recv, ws_send, ws_recv, t_send, t_recv, b_send, b_recv,
 ):
     me = lax.axis_index("dp")
     mt = lax.axis_index("tensor")
     rows, units = w1_ref.shape[1], w1_ref.shape[2]
-    own_count, width = f_ref.shape
+    own_count, width = f_hbm.shape
     count = own_count * tp
     tile = min(256, units)
     tiles = units // tile
@@ -57,11 +58,21 @@
         return flip_rel(rel)
 
     barrier = pltpu.get_barrier_semaphore()
-    for j in range(1, dp):
-        pl.semaphore_signal(barrier, inc=1, device_id={"dp": lax.rem(me + j, dp)}, device_id_type=MESH)
     for j in range(1, tp):
         pl.semaphore_signal(barrier, inc=1, device_id={"tensor": lax.rem(mt + j, tp)}, device_id_type=MESH)
-    pl.semaphore_wait(barrier, dp + tp - 2)
+    for mask in high + [1]:
+        pl.semaphore_signal(barrier, inc=1, device_id={"dp": peer(mask)}, device_id_type=MESH)
+    own_rows = pl.ds(pl.multiple_of(mt * own_count, own_count), own_count)
+    loads = [
+        pltpu.make_async_copy(src, dst, in_sems.at[i])
+        for i, (src, dst) in enumerate((
+            (f_hbm, feats.at[own_rows]), (click_hbm, click_ref), (convert_hbm, convert_ref),
+            (b1_hbm, b1_ref), (w2_hbm, w2_ref),
+        ))
+    ]
+    for copy in loads:
+        copy.start()
+    pl.semaphore_wait(barrier, len(high) + tp)
 
     def block_rows(rel):
         return pl.ds(pl.multiple_of(flip_rel(rel) * rows, rows), rows)
@@ -92,19 +103,21 @@
     for phase in range(len(high)):
         for t in range(2):
             launch(t, 0, orders[t][phase])
-    own_rows = pl.ds(pl.multiple_of(mt * own_count, own_count), own_count)
-    feat_copies = [to_tensor(j, 0, f_ref, feats.at[own_rows]) for j in range(1, tp)]
+    for copy in loads:
+        copy.wait()
+    feat_copies = [to_tensor(j, 0, feats.at[own_rows], feats.at[own_rows]) for j in range(1, tp)]
+    for copy in feat_copies:
+        copy.start()
     lab_copies = [to_tensor(j, 1, labels.at[mt], labels.at[mt]) for j in range(1, tp)]
     click = click_ref[...].astype(F32)
     both = click * convert_ref[...].astype(F32)
     mine = lax.broadcasted_iota(jnp.int32, (1, count), 1) // own_count == mt
     for row, label in enumerate((click, both)):
         labels[mt, row:row + 1, :] = jnp.where(mine, jnp.concatenate([label] * tp, axis=1), 0.0)
-    for copy in feat_copies + lab_copies:
+    for copy in lab_copies:
         copy.start()
     for t in range(2):
         launch(t, 0, 1)
-    feats[own_rows, :] = f_ref[...]
     for t in range(2):
         weights[t, block_rows(0), :] = w1_ref[t]
 
@@ -115,6 +128,9 @@
 
     def multiply(t, group):
         place = pl.ds(pl.multiple_of((flip_rel(group * span) // span) * (span * rows), span * rows), span * rows)
+        multiply_rows(t, place)
+
+    def multiply_rows(t, place):
         opening = not started[t]
         started[t] = True
 
@@ -165,10 +181,17 @@
         label_sum = label_sum + labels[j]
     label_y = label_sum[0:1]
     label_z = label_sum[1:2]
+    def place_of(rel):
+        return pl.ds(pl.multiple_of(flip_rel(rel) * rows, rows), rows)
+
+    split = span == 2 and rows % 128 == 0
+    if split:
+        for t, group in waiting:
+            multiply_rows(t, place_of(group * span))
     for t, group in waiting:
         for rel in range(group * span + 1, (group + 1) * span, 2):
             gathers[t, rel].wait_recv()
-        last = pl.ds(pl.multiple_of((flip_rel(group * span) // span) * (span * rows), span * rows), span * rows)
+        last = place_of(group * span + 1) if split else pl.ds(pl.multiple_of((flip_rel(group * span) // span) * (span * rows), span * rows), span * rows)
 
         def forward(j, total, t=t, last=last):
             cols = pl.ds(pl.multiple_of(j * tile, tile), tile)
@@ -180,18 +203,18 @@
             return total + lax.dot_general(row, hidden, (((1,), (1,)), ((), ())), preferred_element_type=F32)
 
         total = lax.fori_loop(0, tiles, forward, jnp.zeros((16, count), F32))
-        logit_out[t] = total[0:8]
+        logit_out[t:t + 1, :] = total[0:1]
     logit_copies = [to_tensor(j, 2, logit_out, logit_in.at[mt]) for j in range(1, tp)]
     for copy in logit_copies:
         copy.start()
     logit_in[mt] = logit_out[...]
     for copy in logit_copies:
         copy.wait_recv()
-    first = logit_in[0, 0]
-    second = logit_in[0, 1]
+    first = logit_in[0, 0:1]
+    second = logit_in[0, 1:2]
     for j in range(1, tp):
-        first = first + logit_in[j, 0]
-        second = second + logit_in[j, 1]
+        first = first + logit_in[j, 0:1]
+        second = second + logit_in[j, 1:2]
     sa, na = jax.nn.sigmoid(first), jax.nn.sigmoid(-first)
     sb, nb = jax.nn.sigmoid(second), jax.nn.sigmoid(-second)
     q = na + sa * nb
@@ -207,8 +230,8 @@
         -(label_y * na - (1.0 - label_y) * sa) - (label_z * na - shared * na),
         -(label_z * nb - shared * nb),
     )
-    columns = [jnp.transpose(slope)[:, 0:1] for slope in slopes]
-    for t in range(2):
+    columns = [jnp.transpose(jnp.broadcast_to(slope, (8, count)))[:, 0:1] for slope in slopes]
+    def slope_rows(t):
         for j in range(tiles):
             cols = pl.ds(j * tile, tile)
             value = columns[t] * w2_ref[t:t + 1, cols].astype(F32)
@@ -236,6 +259,8 @@
     def to_sibling(step):
         for t in range(2):
             rel = ranked[t][step]
+            if step == 0:
+                slope_rows(t)
             send_sum(t, rel ^ 1, 1, grad_block(t, rel ^ 1))
 
     def reduced(t, rel):
@@ -362,6 +387,7 @@
         lanes = min(128, units)
         chunks = units // lanes
         vmem = pl.BlockSpec(memory_space=pltpu.VMEM)
+        hbm = pl.BlockSpec(memory_space=pltpu.HBM)
         loss, gf, gw, small = pl.pallas_call(
             functools.partial(kernel, dp, tp, scale),
             out_shape=(
@@ -370,15 +396,15 @@
                 jax.ShapeDtypeStruct((rows * chunks * 2, lanes), F32),
                 jax.ShapeDtypeStruct((2, 2, units), F32),
             ),
-            in_specs=[vmem] * 6,
+            in_specs=[hbm, hbm, hbm, vmem, hbm, hbm],
             out_specs=(vmem,) * 4,
             scratch_shapes=[
                 pltpu.VMEM((2, width, units), BF16),
                 pltpu.VMEM((count, width), BF16),
                 pltpu.VMEM((width, count), BF16),
                 pltpu.VMEM((tp, 2, count), F32),
-                pltpu.VMEM((2, 8, count), F32),
-                pltpu.VMEM((tp, 2, 8, count), F32),
+                pltpu.VMEM((2, count), F32),
+                pltpu.VMEM((tp, 2, count), F32),
                 pltpu.VMEM((2, count, units), F32),
                 pltpu.VMEM((2, count, units), BF16),
                 pltpu.VMEM((2, count, units), BF16),
@@ -388,6 +414,11 @@
                 pltpu.VMEM((tp, own_count, width), BF16),
                 pltpu.VMEM((dp.bit_length(), 4, units), F32),
                 pltpu.VMEM((dp.bit_length(), 4, units), F32),
+                pltpu.VMEM((1, own_count), jnp.int32),
+                pltpu.VMEM((1, own_count), jnp.int32),
+                pltpu.VMEM((2, units), F32),
+                pltpu.VMEM((2, units), BF16),
+                pltpu.SemaphoreType.DMA((5,)),
                 pltpu.SemaphoreType.DMA((2, dp)),
                 pltpu.SemaphoreType.DMA((2, dp)),
                 pltpu.SemaphoreType.DMA((2, dp)),

time: 60.1 us -> 60.3 us (level)
  no operation moved by 1% of the time
where the time goes in v3:
time: 60.3 us; the launch traced here: 60.1 us
  Pallas kernels  57.6 us (96%)
  local copies, waits for them, and re-layouts  1.86 us (3%)
  between operations  0.71 us (1%)
    pallas_call x1, Pallas kernels, local(): pl.pallas_call(functools.partial(kernel, dp, tp, scale), out_shape=(jax.S...  56.5 us
    unnamed x11, local copies, waits for them, and re-layouts  1.86 us

profile of v3, /device:TPU:0, one launch (start us, length us, event | category | flops | bytes accessed | tf_op | source)
XLA Modules:
  0.0 60.1 jit_solution(17273458948419422097)
XLA Ops:
  0.6 0.0 copy-start
  0.6 0.0 copy-start.1
  0.7 0.0 copy-start.2
  0.7 1.2 %copy.14 = bf16[128,2,1024]{2,0,1:T(8,128)(2,1)S(1)} copy(bf16[128,2,1024]{2,1,0:T(2,128)(2,1)} %param.9) | data formatting | bytes 1048576 | tf_op args[3]
  1.9 0.0 copy-start.3
  1.9 0.0 copy-start.4
  1.9 0.0 copy-done
  1.9 0.0 copy-done.1
  1.9 0.0 copy-done.2
  1.9 0.6 %copy-done.3 = s32[64]{0:T(128)S(1)} copy-done((s32[64]{0:T(128)S(1)}, s32[64]{0:T(128)}, u32[]{:S(2)}) %copy-start.3) | copy-done | bytes 280
  2.5 0.0 copy-done.4
  2.6 56.5 %shard_map.101 = (f32[1,64]{1,0:T(1,128)S(1)}, bf16[64,1024]{1,0:T(8,128)(2,1)S(1)}, f32[2048,128]{1,0:T(8,128)S(1)}, f32[2,2,1024]{2,1,0:T(2,128)S(1)}) custom-call(bf16[64,1024]{1,0:T(8,128)(2,1)S(1)} %copy-done, s32[1,64]{1,0:T(1,128)S(1)} %bitcast.12, s32[1,64]{1,0:T(1,128)S(1)} %bitcast.13, bf16[2,128,1024]{2,1,0:T(8,128)(2,1)S(1)} %bitcast.11, ...), custom_call_target="tpu_custom_call" | custom-call | tf_op jit(solution)/shard_map/pallas_call | solution.py:391
  59.1 1.1 %shard_map.102 = (f32[1,64]{1,0:T(1,128)}, bf16[64,1024]{1,0:T(8,128)(2,1)}, f32[2048,128]{1,0:T(8,128)}, f32[2,1024]{1,0:T(2,128)}, f32[2,1024]{1,0:T(2,128)}) custom-call(f32[1,64]{1,0:T(1,128)S(1)} %get-tuple-element.14.loss, bf16[64,1024]{1,0:T(8,128)(2,1)S(1)} %get-tuple-element.15.gf, f32[2048,128]{1,0:T(8,128)S(1)} %get-tuple-element.16.gw, ...), custom_call_target="tpu_custom_call" | custom-call | tf_op jit(solution)/shard_map/pallas_call | solution.py:436
Async XLA Ops:
  0.6 1.3 %copy-start = (bf16[64,1024]{1,0:T(8,128)(2,1)S(1)}, bf16[64,1024]{1,0:T(8,128)(2,1)}, u32[]{:S(2)}) copy-start(bf16[64,1024]{1,0:T(8,128)(2,1)} %f_hbm.1) | copy-start | bytes 393220
  0.6 1.3 %copy-start.1 = (f32[2,1024]{1,0:T(2,128)S(1)}, f32[2,1024]{1,0:T(2,128)}, u32[]{:S(2)}) copy-start(f32[2,1024]{1,0:T(2,128)} %b1_hbm.1) | copy-start | bytes 24580
  0.7 1.3 %copy-start.2 = (bf16[2,1024]{1,0:T(2,128)(2,1)S(1)}, bf16[2,1024]{1,0:T(2,128)(2,1)}, u32[]{:S(2)}) copy-start(bf16[2,1024]{1,0:T(2,128)(2,1)} %w2_hbm.1) | copy-start | bytes 12292
  1.9 0.7 %copy-start.3 = (s32[64]{0:T(128)S(1)}, s32[64]{0:T(128)}, u32[]{:S(2)}) copy-start(s32[64]{0:T(128)} %param.7) | copy-start | bytes 772
  1.9 0.7 %copy-start.4 = (s32[64]{0:T(128)S(1)}, s32[64]{0:T(128)}, u32[]{:S(2)}) copy-start(s32[64]{0:T(128)} %param.8) | copy-start | bytes 772
